TPU v7x, 256 devices: a whole 4x4x8 slice. The times are simulated.
256 devices in a mesh: grid: 8 (over z), orb: 16 (over y, x_hi, core), pts: 2 (over x_lo).
Axes of the slice: x: 4 (x_hi: 2, x_lo: 2; x = x_hi * 2 + x_lo), y: 4, z: 8, core: 2. Of those that a mesh axis runs over, the one named last changes fastest.
Arguments:
- orbitals: bfloat16 [2048, 2048], P('grid', 'orb'), may hold values from -6 to 6
- points: int32 [8192], replicated, may hold values from 0 to 2047
- fitting: bfloat16 [2048, 8192], P('grid', ('orb', 'pts')), may hold values from -0.0625 to 0.0625
- screened: bfloat16 [8192, 8192], P(('orb', 'pts'), 'grid'), may hold values from -0.0014648438 to 0.0014648438
Outputs:
- exchange_orbitals: float32 [2048, 2048], P(('orb', 'pts'), 'grid')
- exchange_matrix: float32 [2048, 2048], P(('orb', 'pts'), 'grid')
Inputs may be any that keep to these rules, and one draw needn't show every extreme that they name: Grid rows of the window; two points may name the same row.
All inputs are finite; a program needn't handle non-finite values.
Results may differ from a plain program's by a relative error of at most 0.005.
Values may be sent and summed in bfloat16 or wider, within the bound.
No kernel may reach another device: no remote copies, remote signals or barrier semaphores. Data moves between devices by JAX's collectives and lax.ppermute only.
A program may use at most 128 MiB of HBM per device.

v0:
```python
import math
import jax
import jax.numpy as jnp
from jax import lax
from jax.sharding import PartitionSpec as P


def in_one_piece(arrays, axis, dim, along):
    widths = [a.shape[along] for a in arrays]
    both = jnp.concatenate(arrays, axis=along)
    filled = lax.all_gather(both, axis, axis=dim, tiled=True)
    return tuple(jnp.split(filled, [sum(widths[:k]) for k in range(1, len(widths))], axis=along))


def laid_out(parts, dim):
    parts = jnp.moveaxis(parts, 0, dim)
    shape = parts.shape
    return parts.reshape(*shape[:dim], shape[dim] * shape[dim + 1], *shape[dim + 2 :])


def sent_to_all(x, axis):
    copies = jnp.broadcast_to(x, (lax.axis_size(axis), *x.shape))
    return lax.all_to_all(copies, axis, split_axis=0, concat_axis=0, tiled=True)


def collect(x, axis, dim):
    return laid_out(sent_to_all(x, axis), dim)


def split_up(x, dim, peers):
    shape = x.shape
    parts = x.reshape(*shape[:dim], peers, shape[dim] // peers, *shape[dim + 1 :])
    return jnp.moveaxis(parts, dim, 0)


def sent_and_summed(x, axis, dim):
    peers = lax.axis_size(axis)
    parts = lax.all_to_all(split_up(x, dim, peers), axis, 0, 0, tiled=True)
    return jnp.sum(parts, axis=0)


def per_device(orbitals, points, fitting, screened):
    grid_index = lax.axis_index("grid")
    orb_index = lax.axis_index("orb")
    pts_index = lax.axis_index("pts")
    n_grid = lax.axis_size("grid")
    n_orb = lax.axis_size("orb")
    n_pts = lax.axis_size("pts")
    rows_dev, width_dev = orbitals.shape
    npoints = points.shape[0]
    nfull = width_dev * n_orb
    point_block = npoints // (n_orb * n_pts)
    column_block = npoints // n_grid
    orbital_block = nfull // (n_orb * n_pts)
    local_rows = points - grid_index * rows_dev
    inside = (local_rows >= 0) & (local_rows < rows_dev)
    clamped = jnp.clip(local_rows, 0, rows_dev - 1)
    taken = jnp.take(orbitals, clamped, axis=0).astype(jnp.float32)
    selected = jnp.where(inside[:, None], taken, jnp.zeros_like(taken))
    picked = lax.psum(selected.astype(jnp.bfloat16), "grid")
    grouped = picked.reshape(n_orb, n_pts, point_block, width_dev)
    own_rows = lax.dynamic_index_in_dim(grouped, pts_index, 1, keepdims=False).reshape(
        n_orb * point_block, width_dev
    )
    point_rows = lax.dynamic_slice_in_dim(picked, grid_index * column_block, column_block, 0)
    rows_full, point_full = in_one_piece((own_rows, point_rows), "orb", 1, 0)
    own_full = lax.dynamic_slice_in_dim(rows_full, orb_index * point_block, point_block, 0)
    density = lax.dot_general(
        own_full, point_full, (((1,), (1,)), ((), ())), preferred_element_type=jnp.float32
    )
    masked = (density * screened.astype(jnp.float32)).astype(jnp.bfloat16)
    partial_applied = jnp.dot(masked, point_full, preferred_element_type=jnp.float32)
    applied = lax.psum(partial_applied, "grid").astype(jnp.bfloat16)
    columns = lax.all_to_all(applied, ("orb", "pts"), split_axis=1, concat_axis=0, tiled=True)
    initial = jnp.zeros((orbital_block, rows_dev), jnp.float32)
    terms = initial - lax.dot_general(
        columns,
        lax.all_gather(fitting, ("orb", "pts"), axis=1, tiled=True),
        (((0,), (1,)), ((), ())),
        preferred_element_type=jnp.float32,
    )
    rounded = terms.astype(jnp.bfloat16)
    partial_matrix = jnp.dot(
        rounded, collect(orbitals, "orb", 1), preferred_element_type=jnp.float32
    )
    summed = sent_and_summed(partial_matrix, "grid", 1)
    exchange_matrix = summed / math.sqrt(rows_dev * n_grid)
    return (terms, exchange_matrix)


def solution(mesh):
    in_specs = (P("grid", "orb"), P(), P("grid", ("orb", "pts")), P(("orb", "pts"), "grid"))
    out_specs = (P(("orb", "pts"), "grid"), P(("orb", "pts"), "grid"))
    return jax.shard_map(
        per_device, mesh=mesh, in_specs=in_specs, out_specs=out_specs, check_vma=False
    )
```

profile of v0, /device:TPU:1, one launch (start us, length us, event | category | flops | bytes accessed | tf_op | source)
XLA Modules:
  0.0 432.0 jit_solution(11468976855244154880)
XLA Ops:
  7.2 0.0 copy-start
  7.2 0.0 all-reduce.3.cloned.1.call-start
  7.2 0.8 compare_and_fusion.1
  8.0 0.8 fusion.17
  8.8 0.0 copy-done
  8.8 24.0 %gather_fusion = bf16[8192,128]{1,0:T(8,128)(2,1)S(1)} fusion(bf16[256,128]{1,0:T(8,128)(2,1)S(1)} %copy-done, s32[8192]{0:T(1024)S(1)} %fusion.17), kind=kCustom, calls=%fused_computation | custom fusion | bytes 4227072 | tf_op jit(solution)/shard_map/jit(_take)/gather | solution.py:58
  32.9 6.7 %select_convert_fusion = bf16[8192,128]{1,0:T(8,128)(2,1)} fusion(bf16[8192,128]{1,0:T(8,128)(2,1)S(1)} %gather_fusion, pred[8192]{0:T(1024)(128)(4,1)S(1)} %get-tuple-element.3, pred[8192]{0:T(1024)(128)(4,1)S(1)} %get-tuple-element.2), kind=kLoop, calls=%fused_computation.1 | loop fusion | flops 4194304 | bytes 4210688 | tf_op jit(solution)/shard_map/convert_element_type | solution.py:60
  39.6 0.0 all-reduce.3.cloned.1.call-update
  39.6 0.0 all-gather.3.cloned.1.call-start
  39.7 82.1 %all-reduce.3.cloned.1.call-done = bf16[8192,128]{1,0:T(8,128)(2,1)} async-done(((bf16[8192,128]{1,0:T(8,128)(2,1)}), bf16[8192,128]{1,0:T(8,128)(2,1)}) %all-reduce.3.cloned.1.call-update) | async-done | bytes 2097168 | tf_op jit(solution)/shard_map/psum | solution.py:60
  121.8 1.3 constant_dynamic-slice_fusion.1
  123.1 1.0 constant_dynamic-slice_fusion
  124.1 1.2 pad_maximum_fusion
  125.2 0.0 all-gather.3.cloned.1.call-update
  125.3 0.0 all-gather.5.cloned.1.call-start
  125.3 0.7 all-gather.5.cloned.1.call-update
  126.0 0.0 copy-start.2
  126.0 147.0 %all-gather.3.cloned.1.call-done = bf16[5120,2048]{1,0:T(8,128)(2,1)} async-done(((bf16[5120,128]{1,0:T(8,128)(2,1)}), bf16[5120,2048]{1,0:T(8,128)(2,1)}) %all-gather.3.cloned.1.call-update) | async-done | bytes 20971536 | tf_op jit(solution)/shard_map/all_gather | solution.py:11
  273.0 14.2 %split.8 = bf16[4096,2048]{1,0:T(8,128)(2,1)} slice(bf16[5120,2048]{1,0:T(8,128)(2,1)} %all-gather.3.cloned.1.call-done), slice={[0:4096], [0:2048]} | slice | bytes 33554432 | tf_op jit(solution)/shard_map/split | solution.py:12
  287.2 0.0 copy-done.2
  287.2 6.2 %fusion = f32[256,2048]{1,0:T(8,128)S(1)} fusion(bf16[5120,2048]{1,0:T(8,128)(2,1)} %all-gather.3.cloned.1.call-done, bf16[256,1024]{1,0:T(8,128)(2,1)S(1)} %copy-done.2, bf16[4096,2048]{1,0:T(8,128)(2,1)} %split.8, s32[]{:T(128)S(6)} %select_n.28), kind=kOutput, calls=%fused_computation.2 | convolution fusion | flops 2148270080 | bytes 12058628 | tf_op jit(solution)/shard_map/dot_general | solution.py:72
  293.5 55.7 %all-reduce.4 = bf16[256,2048]{1,0:T(8,128)(2,1)S(1)} all-reduce(f32[256,2048]{1,0:T(8,128)S(1)} %fusion), channel_id=1, replica_groups=mesh['grid'=8,'orb'=16,'pts'=2] {'grid'}, use_global_device_ids=true, to_apply=%region_1.2 | all-reduce | flops 524288 | bytes 3145728 | tf_op jit(solution)/shard_map/psum | solution.py:73
  349.2 1.3 copy.7
  350.5 15.2 %all-to-all-start = ((bf16[256,32,64]{0,2,1:T(8,128)(2,1)}), bf16[256,32,64]{0,2,1:T(8,128)(2,1)S(1)}, u32[]{:S(2)}, u32[]{:S(2)}) async-start(bf16[256,32,64]{0,2,1:T(8,128)(2,1)} %bitcast.2), calls=%async_computation | async-start | bytes 2097152 | tf_op jit(solution)/shard_map/all_to_all | solution.py:74
  365.7 0.1 copy.9
  365.8 15.6 %all-to-all-done = bf16[256,32,64]{0,2,1:T(8,128)(2,1)S(1)} async-done(((bf16[256,32,64]{0,2,1:T(8,128)(2,1)}), bf16[256,32,64]{0,2,1:T(8,128)(2,1)S(1)}, u32[]{:S(2)}, u32[]{:S(2)}) %all-to-all-start) | async-done | bytes 1048608 | tf_op jit(solution)/shard_map/all_to_all | solution.py:74
  381.4 1.1 broadcast_in_dim.36
  382.5 6.0 %all-to-all-start.1 = ((bf16[16,256,128]{1,2,0:T(8,128)(2,1)}), bf16[16,256,128]{1,2,0:T(8,128)(2,1)S(1)}, u32[]{:S(2)}, u32[]{:S(2)}) async-start(bf16[16,256,128]{1,2,0:T(8,128)(2,1)} %broadcast_in_dim.36), calls=%async_computation.1 | async-start | bytes 2097152 | tf_op jit(solution)/shard_map/all_to_all | solution.py:23
  388.5 0.1 copy.10
  388.6 0.0 all-gather.5.cloned.1.call-done
  388.6 3.6 convolution_subtract_fusion
  392.2 0.0 copy-start.1
  392.2 13.4 %all-to-all-done.1 = bf16[16,256,128]{1,2,0:T(8,128)(2,1)S(1)} async-done(((bf16[16,256,128]{1,2,0:T(8,128)(2,1)}), bf16[16,256,128]{1,2,0:T(8,128)(2,1)S(1)}, u32[]{:S(2)}, u32[]{:S(2)}) %all-to-all-start.1) | async-done | bytes 1048608 | tf_op jit(solution)/shard_map/all_to_all | solution.py:23
  405.6 0.4 convolution_bitcast_fusion
  406.0 18.8 %all_to_all.29 = f32[8,64,256]{2,1,0:T(8,128)S(1)} all-to-all(f32[8,64,256]{2,1,0:T(8,128)S(1)} %convolution_bitcast_fusion), channel_id=1, replica_groups=mesh['grid'=8,'orb'=16,'pts'=2] {'grid'}, dimensions={0} | all-to-all | bytes 1048576 | tf_op jit(solution)/shard_map/all_to_all | solution.py:38
  424.9 0.6 broadcast_multiply_fusion
  425.5 0.0 copy-done.1
  (1 shorter events, 0.0 us)
Async XLA Ops:
  7.2 1.6 copy-start
  7.2 114.6 %all-reduce.3.cloned.1.call-start = ((), (), s32[]{:S(2)}) async-start(), calls=%async_computation.3 | async-start | bytes 4194304 | tf_op jit(solution)/shard_map/psum | solution.py:60
  39.6 233.4 %all-gather.3.cloned.1.call-start = ((), (), s32[]{:S(2)}) async-start(), calls=%async_computation.4 | async-start | bytes 22282240 | tf_op jit(solution)/shard_map/all_gather | solution.py:11
  125.3 263.3 %all-gather.5.cloned.1.call-start = ((), (), s32[]{:S(2)}) async-start(), calls=%async_computation.5 | async-start | bytes 4325376 | tf_op jit(solution)/shard_map/all_gather | solution.py:78
  126.0 161.3 %copy-start.2 = (bf16[256,1024]{1,0:T(8,128)(2,1)S(1)}, bf16[256,1024]{1,0:T(8,128)(2,1)}, u32[]{:S(2)}) copy-start(bf16[256,1024]{1,0:T(8,128)(2,1)} %param.7) | copy-start | bytes 1572868
  350.5 30.9 %all-to-all-start = ((bf16[256,32,64]{0,2,1:T(8,128)(2,1)}), bf16[256,32,64]{0,2,1:T(8,128)(2,1)S(1)}, u32[]{:S(2)}, u32[]{:S(2)}) async-start(bf16[256,32,64]{0,2,1:T(8,128)(2,1)} %bitcast.2), calls=%async_computation | async-start | bytes 2097152 | tf_op jit(solution)/shard_map/all_to_all | solution.py:74
  382.5 23.1 %all-to-all-start.1 = ((bf16[16,256,128]{1,2,0:T(8,128)(2,1)}), bf16[16,256,128]{1,2,0:T(8,128)(2,1)S(1)}, u32[]{:S(2)}, u32[]{:S(2)}) async-start(bf16[16,256,128]{1,2,0:T(8,128)(2,1)} %broadcast_in_dim.36), calls=%async_computation.1 | async-start | bytes 2097152 | tf_op jit(solution)/shard_map/all_to_all | solution.py:23
  392.2 33.3 %copy-start.1 = (f32[64,256]{1,0:T(8,128)}, f32[64,256]{1,0:T(8,128)S(1)}, u32[]{:S(2)}) copy-start(f32[64,256]{1,0:T(8,128)S(1)} %convolution_subtract_fusion) | copy-start | bytes 196612
Sparse Core Ops, SparseCore 0:
  39.7 82.0 all-reduce.2
  125.4 147.6 all-gather.2
  274.8 82.4 all-gather.4
where the time goes:
time: 433 us; the launch traced here: 432 us
  waiting for transfers between devices  259 us (60%)
  blocking collectives  74.5 us (17%)
  local copies, waits for them, and re-layouts  43.1 us (10%)
  starting transfers between devices  21.3 us (5%)
  between operations  13.9 us (3%)
  matrix products  10.2 us (2%)
  other arithmetic  10.1 us (2%)
    all_gather x1, waiting for transfers between devices, in_one_piece(): filled = lax.all_gather(both, axis, axis=dim, tiled=True)  147 us
    psum x1, waiting for transfers between devices, per_device(): picked = lax.psum(selected.astype(jnp.bfloat16), 'grid')  82.1 us
    psum x1, blocking collectives, per_device(): applied = lax.psum(partial_applied, 'grid').astype(jnp.bfloat16)  55.7 us
    gather x1, local copies, waits for them, and re-layouts, per_device(): taken = jnp.take(orbitals, clamped, axis=0).astype(jnp.float32)  24 us
    all_to_all x1, blocking collectives, sent_and_summed(): parts = lax.all_to_all(split_up(x, dim, peers), axis, 0, 0, tiled=True)  18.8 us
    all_to_all x1, waiting for transfers between devices, per_device(): lax.all_to_all(applied, ('orb', 'pts'), split_axis=1, concat_axis=0, tile...  15.6 us
    all_to_all x1, starting transfers between devices, per_device(): lax.all_to_all(applied, ('orb', 'pts'), split_axis=1, concat_axis=0, tile...  15.2 us
    split x1, local copies, waits for them, and re-layouts, in_one_piece(): jnp.split(filled, [sum(widths[:k]) for k in range(1, len(widths))], axis=...  14.2 us
  transfers between devices with their start and end apart: 5, of which 4 were waited for; matrix products, arithmetic and copies ran while one was open for 6% of the time, Pallas kernels for 0%

commit v1 on v0

--- a/solution.py
+++ b/solution.py
@@ -70,7 +70,7 @@
     )
     masked = (density * screened.astype(jnp.float32)).astype(jnp.bfloat16)
     partial_applied = jnp.dot(masked, point_full, preferred_element_type=jnp.float32)
-    applied = lax.psum(partial_applied, "grid").astype(jnp.bfloat16)
+    applied = jnp.sum(lax.all_gather(partial_applied, "grid"), 0).astype(jnp.bfloat16)
     columns = lax.all_to_all(applied, ("orb", "pts"), split_axis=1, concat_axis=0, tiled=True)
     initial = jnp.zeros((orbital_block, rows_dev), jnp.float32)
     terms = initial - lax.dot_general(

time: 433 us -> 602 us (1.39)
  waiting for transfers between devices: 259 us -> 478 us
  blocking collectives: 74.5 us -> 21.8 us
  other arithmetic: 10.1 us -> 17.9 us
    all_gather x0 -> x1, waiting for transfers between devices: none -> 169 us  [per_device(): lax.all_gather(partial_applied, 'grid')]
    all_gather x1, waiting for transfers between devices: 0.02 us -> 62.9 us  [per_device(): lax.all_gather(fitting, ('orb', 'pts'), axis=1, tiled=True)]
    psum x1 -> x0, blocking collectives: 55.7 us -> none  [per_device(): applied = lax.psum(partial_applied, 'grid').astype(jnp.bfloat16)]
    all_to_all x1, waiting for transfers between devices: 13.4 us -> 0.01 us  [sent_to_all(): return lax.all_to_all(copies, axis, split_axis=0, concat_axis=0, tiled=True)]
    reduce_sum x0 -> x1, other arithmetic: none -> 7.76 us  [per_device(): jnp.sum(lax.all_gather(partial_applied, 'grid'), 0).astype(jnp.bfloat16)]
    all_to_all x1, starting transfers between devices: 15.2 us -> 7.7 us  [per_device(): lax.all_to_all(applied, ('orb', 'pts'), split_axis=1, concat_axis=0, tile...]
  transfers between devices with their start and end apart: 5 -> 6, of which waited for: 4 -> 5; matrix products, arithmetic and copies ran while one was open for 6% -> 2% of each run, Pallas kernels for 0% -> 0%
where the time goes in v1:
time: 602 us; the launch traced here: 601 us
  waiting for transfers between devices  478 us (79%)
  local copies, waits for them, and re-layouts  43.1 us (7%)
  blocking collectives  21.8 us (4%)
  other arithmetic  17.9 us (3%)
  starting transfers between devices  15.4 us (3%)
  between operations  13.9 us (2%)
  matrix products  11.5 us (2%)
    all_gather x1, waiting for transfers between devices, per_device(): lax.all_gather(partial_applied, 'grid')  169 us
    all_gather x1, waiting for transfers between devices, in_one_piece(): filled = lax.all_gather(both, axis, axis=dim, tiled=True)  148 us
    psum x1, waiting for transfers between devices, per_device(): picked = lax.psum(selected.astype(jnp.bfloat16), 'grid')  82.1 us
    all_gather x1, waiting for transfers between devices, per_device(): lax.all_gather(fitting, ('orb', 'pts'), axis=1, tiled=True)  62.9 us
    gather x1, local copies, waits for them, and re-layouts, per_device(): taken = jnp.take(orbitals, clamped, axis=0).astype(jnp.float32)  24 us
    all_to_all x1, blocking collectives, sent_and_summed(): parts = lax.all_to_all(split_up(x, dim, peers), axis, 0, 0, tiled=True)  21.8 us
    all_to_all x1, waiting for transfers between devices, per_device(): lax.all_to_all(applied, ('orb', 'pts'), split_axis=1, concat_axis=0, tile...  15.5 us
    split x1, local copies, waits for them, and re-layouts, in_one_piece(): jnp.split(filled, [sum(widths[:k]) for k in range(1, len(widths))], axis=...  14.2 us
  transfers between devices with their start and end apart: 6, of which 5 were waited for; matrix products, arithmetic and copies ran while one was open for 2% of the time, Pallas kernels for 0%

profile of v1, /device:TPU:1, one launch (start us, length us, event | category | flops | bytes accessed | tf_op | source)
XLA Modules:
  0.0 601.4 jit_solution(1006111958226428812)
XLA Ops:
  7.2 0.0 copy-start
  7.2 0.0 all-reduce.2.cloned.1.call-start
  7.2 0.8 compare_and_fusion.1
  8.0 0.8 fusion.17
  8.8 0.0 copy-done
  8.8 24.0 %gather_fusion = bf16[8192,128]{1,0:T(8,128)(2,1)S(1)} fusion(bf16[256,128]{1,0:T(8,128)(2,1)S(1)} %copy-done, s32[8192]{0:T(1024)S(1)} %fusion.17), kind=kCustom, calls=%fused_computation | custom fusion | bytes 4227072 | tf_op jit(solution)/shard_map/jit(_take)/gather | solution.py:58
  32.9 6.7 %select_convert_fusion = bf16[8192,128]{1,0:T(8,128)(2,1)} fusion(bf16[8192,128]{1,0:T(8,128)(2,1)S(1)} %gather_fusion, pred[8192]{0:T(1024)(128)(4,1)S(1)} %get-tuple-element.3, pred[8192]{0:T(1024)(128)(4,1)S(1)} %get-tuple-element.2), kind=kLoop, calls=%fused_computation.1 | loop fusion | flops 4194304 | bytes 4210688 | tf_op jit(solution)/shard_map/convert_element_type | solution.py:60
  39.6 0.0 all-reduce.2.cloned.1.call-update
  39.6 0.0 all-gather.5.cloned.1.call-start
  39.7 82.1 %all-reduce.2.cloned.1.call-done = bf16[8192,128]{1,0:T(8,128)(2,1)} async-done(((bf16[8192,128]{1,0:T(8,128)(2,1)}), bf16[8192,128]{1,0:T(8,128)(2,1)}) %all-reduce.2.cloned.1.call-update) | async-done | bytes 2097168 | tf_op jit(solution)/shard_map/psum | solution.py:60
  121.8 1.3 constant_dynamic-slice_fusion.1
  123.1 1.0 constant_dynamic-slice_fusion
  124.1 1.2 pad_maximum_fusion
  125.2 0.0 all-gather.5.cloned.1.call-update
  125.2 0.0 all-gather.9.cloned.1.call-start
  125.3 0.0 copy-start.2
  125.3 147.7 %all-gather.5.cloned.1.call-done = bf16[5120,2048]{1,0:T(8,128)(2,1)} async-done(((bf16[5120,128]{1,0:T(8,128)(2,1)}), bf16[5120,2048]{1,0:T(8,128)(2,1)}) %all-gather.5.cloned.1.call-update) | async-done | bytes 20971536 | tf_op jit(solution)/shard_map/all_gather | solution.py:11
  273.0 14.2 %split.8 = bf16[4096,2048]{1,0:T(8,128)(2,1)} slice(bf16[5120,2048]{1,0:T(8,128)(2,1)} %all-gather.5.cloned.1.call-done), slice={[0:4096], [0:2048]} | slice | bytes 33554432 | tf_op jit(solution)/shard_map/split | solution.py:12
  287.2 0.0 copy-done.2
  287.2 7.4 %fusion = f32[256,2048]{1,0:T(8,128)} fusion(bf16[5120,2048]{1,0:T(8,128)(2,1)} %all-gather.5.cloned.1.call-done, bf16[256,1024]{1,0:T(8,128)(2,1)S(1)} %copy-done.2, bf16[4096,2048]{1,0:T(8,128)(2,1)} %split.8, s32[]{:T(128)S(6)} %select_n.28), kind=kOutput, calls=%fused_computation.2 | convolution fusion | flops 2148270080 | bytes 12058628 | tf_op jit(solution)/shard_map/dot_general | solution.py:72
  294.7 0.0 all-gather.9.cloned.1.call-update
  294.7 0.0 all-gather.7.cloned.1.call-start
  294.7 0.5 all-gather.7.cloned.1.call-update
  295.3 169.0 %all-gather.9.cloned.1.call-done = f32[2048,2048]{1,0:T(8,128)} async-done(((f32[256,2048]{1,0:T(8,128)}), f32[2048,2048]{1,0:T(8,128)}) %all-gather.9.cloned.1.call-update) | async-done | bytes 16777232 | tf_op jit(solution)/shard_map/all_gather | solution.py:73
  464.3 7.8 %reduce_sum.18 = bf16[256,2048]{1,0:T(8,128)(2,1)S(1)} reduce(f32[8,256,2048]{2,1,0:T(8,128)} %bitcast.22, f32[]{:T(128)} %constant.14.clone.1), dimensions={0}, to_apply=%region_1.2 | reduce | flops 3670016 | bytes 17825796 | tf_op jit(solution)/shard_map/reduce_sum | solution.py:73
  472.1 1.3 copy.9
  473.4 7.7 %all-to-all-start = ((bf16[256,32,64]{0,2,1:T(8,128)(2,1)}), bf16[256,32,64]{0,2,1:T(8,128)(2,1)S(1)}, u32[]{:S(2)}, u32[]{:S(2)}) async-start(bf16[256,32,64]{0,2,1:T(8,128)(2,1)} %bitcast.3), calls=%async_computation | async-start | bytes 2097152 | tf_op jit(solution)/shard_map/all_to_all | solution.py:74
  481.1 0.1 copy.11
  481.2 15.5 %all-to-all-done = bf16[256,32,64]{0,2,1:T(8,128)(2,1)S(1)} async-done(((bf16[256,32,64]{0,2,1:T(8,128)(2,1)}), bf16[256,32,64]{0,2,1:T(8,128)(2,1)S(1)}, u32[]{:S(2)}, u32[]{:S(2)}) %all-to-all-start) | async-done | bytes 1048608 | tf_op jit(solution)/shard_map/all_to_all | solution.py:74
  496.7 1.1 broadcast_in_dim.36
  497.7 7.6 %all-to-all-start.1 = ((bf16[16,256,128]{1,2,0:T(8,128)(2,1)}), bf16[16,256,128]{1,2,0:T(8,128)(2,1)S(1)}, u32[]{:S(2)}, u32[]{:S(2)}) async-start(bf16[16,256,128]{1,2,0:T(8,128)(2,1)} %broadcast_in_dim.36), calls=%async_computation.1 | async-start | bytes 2097152 | tf_op jit(solution)/shard_map/all_to_all | solution.py:23
  505.3 0.1 copy.12
  505.4 62.9 %all-gather.7.cloned.1.call-done = bf16[256,8192]{1,0:T(8,128)(2,1)} async-done(((bf16[256,256]{1,0:T(8,128)(2,1)}), bf16[256,8192]{1,0:T(8,128)(2,1)}) %all-gather.7.cloned.1.call-update) | async-done | bytes 4194320 | tf_op jit(solution)/shard_map/all_gather | solution.py:78
  568.3 3.6 convolution_subtract_fusion
  571.9 0.0 copy-start.1
  571.9 0.0 all-to-all-done.1
  571.9 0.4 convolution_bitcast_fusion
  572.3 21.8 %all_to_all.26 = f32[8,64,256]{2,1,0:T(8,128)S(1)} all-to-all(f32[8,64,256]{2,1,0:T(8,128)S(1)} %convolution_bitcast_fusion), channel_id=1, replica_groups=mesh['grid'=8,'orb'=16,'pts'=2] {'grid'}, dimensions={0} | all-to-all | bytes 1048576 | tf_op jit(solution)/shard_map/all_to_all | solution.py:38
  594.2 0.6 broadcast_multiply_fusion
  594.8 0.0 copy-done.1
  (1 shorter events, 0.0 us)
Async XLA Ops:
  7.2 1.6 copy-start
  7.2 114.6 %all-reduce.2.cloned.1.call-start = ((), (), s32[]{:S(2)}) async-start(), calls=%async_computation.3 | async-start | bytes 4194304 | tf_op jit(solution)/shard_map/psum | solution.py:60
  39.6 233.4 %all-gather.5.cloned.1.call-start = ((), (), s32[]{:S(2)}) async-start(), calls=%async_computation.4 | async-start | bytes 22282240 | tf_op jit(solution)/shard_map/all_gather | solution.py:11
  125.2 339.0 %all-gather.9.cloned.1.call-start = ((), (), s32[]{:S(2)}) async-start(), calls=%async_computation.6 | async-start | bytes 18874368 | tf_op jit(solution)/shard_map/all_gather | solution.py:73
  125.3 161.9 %copy-start.2 = (bf16[256,1024]{1,0:T(8,128)(2,1)S(1)}, bf16[256,1024]{1,0:T(8,128)(2,1)}, u32[]{:S(2)}) copy-start(bf16[256,1024]{1,0:T(8,128)(2,1)} %param.7) | copy-start | bytes 1572868
  294.7 273.6 %all-gather.7.cloned.1.call-start = ((), (), s32[]{:S(2)}) async-start(), calls=%async_computation.5 | async-start | bytes 4325376 | tf_op jit(solution)/shard_map/all_gather | solution.py:78
  473.4 23.3 %all-to-all-start = ((bf16[256,32,64]{0,2,1:T(8,128)(2,1)}), bf16[256,32,64]{0,2,1:T(8,128)(2,1)S(1)}, u32[]{:S(2)}, u32[]{:S(2)}) async-start(bf16[256,32,64]{0,2,1:T(8,128)(2,1)} %bitcast.3), calls=%async_computation | async-start | bytes 2097152 | tf_op jit(solution)/shard_map/all_to_all | solution.py:74
  497.7 74.1 %all-to-all-start.1 = ((bf16[16,256,128]{1,2,0:T(8,128)(2,1)}), bf16[16,256,128]{1,2,0:T(8,128)(2,1)S(1)}, u32[]{:S(2)}, u32[]{:S(2)}) async-start(bf16[16,256,128]{1,2,0:T(8,128)(2,1)} %broadcast_in_dim.36), calls=%async_computation.1 | async-start | bytes 2097152 | tf_op jit(solution)/shard_map/all_to_all | solution.py:23
  571.9 23.0 %copy-start.1 = (f32[64,256]{1,0:T(8,128)}, f32[64,256]{1,0:T(8,128)S(1)}, u32[]{:S(2)}) copy-start(f32[64,256]{1,0:T(8,128)S(1)} %convolution_subtract_fusion) | copy-start | bytes 196612
Sparse Core Ops, SparseCore 0:
  39.7 82.0 all-reduce.1
  125.4 147.6 all-gather.4
  294.8 169.4 all-gather.8
  465.9 102.3 all-gather.6
